TPU v7x, 32 devices: a whole 2x2x4 slice. The times are simulated.
32 devices in a mesh: prow: 4 (over z), pcol: 8 (over y, x, core).
Axes of the slice: x: 2, y: 2, z: 4, core: 2. Of those that a mesh axis runs over, the one named last changes fastest.
Arguments:
- points: float32 [1, 8, 2, 1024], P(None, 'pcol'), may hold values from 0 to 1
- range_length: float32 [1], replicated, may hold values from 0.05 to 0.15
- smoothness: int32 [1], replicated, may hold values from 0 to 2
- sketch_bank: bfloat16 [8, 48, 1024], P('pcol'), may hold values from -6 to 6
- sketch_ids: int32 [2, 4, 1, 8], P(None, 'prow', None, 'pcol'), may hold values from 0 to 7
- tile_ranks: int32 [2, 4, 1, 8], P(None, 'prow', None, 'pcol'), may hold values from 16 to 48
Outputs:
- y_factors: float32 [2, 4, 1, 8, 48, 1024], P(None, 'prow', None, 'pcol')
- c_factors: float32 [2, 4, 1, 8, 48, 1024], P(None, 'prow', None, 'pcol')
- tile_error: float32 [2, 4, 1, 8], P(None, 'prow', None, 'pcol')
- rank_total: int32 [1], replicated
All inputs are finite; a program needn't handle non-finite values.
Results may differ from a plain program's by a relative error of at most 0.0098.
The roundings to bfloat16 on the way count: a program that leaves them out, or rounds other values in their place, can miss the bound.
Values may be sent and summed in bfloat16 or wider, within the bound.
A program may use at most 64 MiB of HBM per device.

v0:
```python
import jax
import jax.numpy as jnp
from jax import lax
from jax.sharding import PartitionSpec as P


def kernel_factors(smoothness, range_length):
    morton_value = smoothness[0].astype(jnp.float32)
    kernel_scale = jnp.sqrt(2.0 * morton_value + 1.0) / range_length[0]
    linear_factor = jnp.where(smoothness[0] >= 1, 1.0, 0.0).astype(jnp.float32)
    squared_distance = jnp.where(smoothness[0] >= 2, 1.0 / 3.0, 0.0).astype(jnp.float32)
    return (kernel_scale, linear_factor, squared_distance)


def covariance_tile(row_locations, column_locations, kernel_scale, linear_factor, squared_distance):
    offset_horizontal = row_locations[0][:, None] - column_locations[0][None, :]
    offset_vertical = row_locations[1][:, None] - column_locations[1][None, :]
    scaled_distance = kernel_scale * jnp.sqrt(
        offset_horizontal * offset_horizontal + offset_vertical * offset_vertical
    )
    return (
        1.0 + linear_factor * scaled_distance + squared_distance * scaled_distance * scaled_distance
    ) * jnp.exp(-scaled_distance)


def compress(tile_low, sketch, rank):
    keep = jnp.arange(sketch.shape[0]) < rank
    sketch = jnp.where(keep[:, None], sketch, jnp.zeros_like(sketch))
    sketched = lax.dot_general(
        sketch, tile_low, (((1,), (1,)), ((), ())), preferred_element_type=jnp.float32
    )
    product = jnp.dot(sketched.astype(jnp.bfloat16), tile_low, preferred_element_type=jnp.float32)
    gram = jnp.dot(sketched, sketched.T, precision=lax.Precision.HIGHEST)
    shift = 0.1 * jnp.trace(gram) / rank.astype(jnp.float32)
    gram = gram + jnp.diag(jnp.where(keep, shift, jnp.ones_like(shift)))
    factor = jnp.linalg.cholesky(gram)
    coeffs = jax.scipy.linalg.cho_solve((factor, True), product)
    approx = lax.dot_general(
        sketched, coeffs, (((0,), (0,)), ((), ())), precision=lax.Precision.HIGHEST
    )
    error = tile_low.astype(jnp.float32) - approx
    return (sketched, coeffs, jnp.sum(error * error))


def per_device(points, range_length, smoothness, sketch_bank, sketch_ids, tile_ranks):
    row_count = lax.axis_size("prow")
    col_count = lax.axis_size("pcol")
    row_place = lax.axis_index("prow")
    col_place = lax.axis_index("pcol")
    row_tiles = sketch_ids.shape[0]
    col_tiles = sketch_ids.shape[2]
    tile_size = points.shape[3]
    sketch_rows = sketch_bank.shape[1]
    slots_total = row_tiles * col_tiles
    tiles_across = col_tiles * col_count
    kernel_scale, linear_factor, squared_distance = kernel_factors(smoothness, range_length)
    gathered = lax.all_gather(points, "pcol", axis=1, tiled=True)
    every_block = gathered.reshape(tiles_across, 2, tile_size)
    row_index = jnp.arange(row_tiles, dtype=jnp.int32) * row_count + row_place
    col_index = jnp.arange(col_tiles, dtype=jnp.int32) * col_count + col_place
    slot_row = jnp.repeat(row_index, col_tiles)
    slot_col = jnp.tile(col_index, row_tiles)
    own_ids = sketch_ids.reshape(slots_total)
    own_ranks = tile_ranks.reshape(slots_total)
    lower = slot_col <= slot_row
    offdiag = slot_col < slot_row
    ranks_local = jnp.sum(jnp.where(offdiag, own_ranks, 0))
    rank_sum = lax.psum(ranks_local, ("prow", "pcol"))
    bank_whole = lax.all_gather(sketch_bank, "pcol", axis=0, tiled=True)
    chosen = bank_whole[own_ids]
    row_points_all = every_block[slot_row]
    col_points_all = every_block[slot_col]

    def one_tile(row_locations, column_locations, sketch, rank):
        tile_block = covariance_tile(
            row_locations, column_locations, kernel_scale, linear_factor, squared_distance
        )
        norm_sq = jnp.sum(tile_block * tile_block)
        sketched, coeffs, err_sq = compress(tile_block.astype(jnp.bfloat16), sketch, rank)
        return (sketched, coeffs, norm_sq, err_sq)

    def mapped(inputs):
        return one_tile(inputs[0], inputs[1], inputs[2], inputs[3])

    sketched_all, coeffs_all, norm_all, err_all = lax.map(
        mapped, (row_points_all, col_points_all, chosen, own_ranks)
    )
    norm_local = jnp.sum(jnp.where(lower, jnp.where(offdiag, 2.0, 1.0) * norm_all, 0.0))
    total = lax.psum(norm_local, ("prow", "pcol"))
    errors = (
        jnp.where(offdiag, jnp.sqrt(err_all), jnp.sqrt(norm_all)) * tiles_across / jnp.sqrt(total)
    )
    errors = jnp.where(lower, errors, 0.0)
    out_shape = (row_tiles, 1, col_tiles, 1, sketch_rows, tile_size)
    y_out = jnp.where(offdiag[:, None, None], sketched_all, 0.0).reshape(out_shape)
    c_out = jnp.where(offdiag[:, None, None], coeffs_all, 0.0).reshape(out_shape)
    err_out = errors.reshape(row_tiles, 1, col_tiles, 1)
    rank_out = rank_sum.reshape(1)
    return (y_out, c_out, err_out, rank_out)


def solution(mesh):
    in_specs = (
        P(None, "pcol", None, None),
        P(),
        P(),
        P("pcol", None, None),
        P(None, "prow", None, "pcol"),
        P(None, "prow", None, "pcol"),
    )
    out_specs = (
        P(None, "prow", None, "pcol", None, None),
        P(None, "prow", None, "pcol", None, None),
        P(None, "prow", None, "pcol"),
        P(),
    )
    return jax.shard_map(
        per_device, mesh=mesh, in_specs=in_specs, out_specs=out_specs, check_vma=False
    )
```

profile of v0, /device:TPU:0, one launch (start us, length us, event | category | flops | bytes accessed | tf_op | source)
XLA Modules:
  0.0 177.8 jit_solution(8479940237843029648)
XLA Ops:
  0.7 10.9 %all_gather.7 = f32[1,8,2,1024]{3,2,0,1:T(2,128)S(1)} all-gather(f32[1,1,2,1024]{3,2,0,1:T(2,128)} %bitcast.135), channel_id=1, replica_groups=mesh['prow'=4,'pcol'=8] {'pcol'}, dimensions={1}, use_global_device_ids=true | all-gather | bytes 73728 | tf_op jit(solution)/shard_map/all_gather | solution.py:57
  14.1 10.2 %all_gather.6 = bf16[8,48,1024]{2,1,0:T(8,128)(2,1)S(1)} all-gather(bf16[1,48,1024]{2,1,0:T(8,128)(2,1)} %param.11), channel_id=1, replica_groups=mesh['prow'=4,'pcol'=8] {'pcol'}, dimensions={0}, use_global_device_ids=true | all-gather | bytes 884736 | tf_op jit(solution)/shard_map/all_gather | solution.py:69
  25.0 68.5 %while.17 = (s32[]{:T(128)}, f32[2,48,1024]{2,1,0:T(8,128)S(1)}, f32[2,48,1024]{2,1,0:T(8,128)S(1)}, f32[2]{0:T(128)S(1)}, f32[2]{0:T(128)S(1)}, /*index=5*/s32[...) while((s32[]{:T(128)}, f32[2,48,1024]{2,1,0:T(8,128)S(1)}, ...), condition=%wide.region_6.7_spmd.clone, body=%wide.region_0.6_spmd.sunk.clone | while | flops 954344128 | bytes 2676799 | solution.py:85
  26.5 3.2 %bitcast_dynamic-update-slice_fusion.6 = (f32[2,48,1024]{2,1,0:T(8,128)S(1)}, f32[48,1024]{1,0:T(8,128)S(1)}) fusion(f32[2,48,1024]{2,1,0:T(8,128)S(1)} %get-tuple-element.256, s32[]{:T(128)} %get-tuple-element.255, f32[]{:T(128)} %get-tuple-element.278, f32[1024]{0:T(1024)S(1)} %bitcast.123, f32[1024]{0:T(1024)S(1)} %bitcast.127, ...), kind=kOutput, calls=%fused_computation.12.clone.1.clone | convolution fusion | flops 115392512 | bytes 510976 | tf_op jit(solution)/shard_map/while/body/eval_jaxpr/dot_general | solution.py:29
  29.6 0.9 select_reduce_fusion.7
  32.7 4.4 %cholesky.73 = f32[48,48]{1,0:T(8,128)S(1)} custom-call(f32[48,48]{1,0:T(8,128)S(1)} %fusion.68), custom_call_target="Cholesky" | custom-call | tf_op jit(solution)/shard_map/while/body/eval_jaxpr/jit(cholesky)/cholesky | solution.py:36
  38.5 3.7 %custom-call.20 = f32[1,48,48]{1,2,0:T(8,128)S(1)} custom-call(f32[1,48,48]{2,1,0:T(8,128)S(1)} %fusion.69), custom_call_target="InvertDiagBlocksLowerTriangular" | custom-call | tf_op jit(solution)/shard_map/while/body/eval_jaxpr/jit(_cho_solve)/triangular_solve | solution.py:37
  42.2 3.2 %fusion.67 = f32[48,1024]{1,0:T(8,128)S(1)} fusion(f32[]{:T(128)} %get-tuple-element.278, f32[1024]{0:T(1024)S(1)} %bitcast.124, f32[1024]{0:T(1024)S(1)} %bitcast.128, f32[1024]{0:T(1024)S(1)} %bitcast.120, f32[1024]{0:T(1024)S(1)} %bitcast.132, f32[]{:T(128)} %get-tuple-element.275, f32[]{:T(128)} %get-tuple-element.274, ...), kind=kOutput, calls=%fused_computation.9.clone.1.clone | convolution fusion | flops 115392512 | bytes 409612 | tf_op jit(solution)/shard_map/while/body/eval_jaxpr/dot_general | solution.py:32
  46.1 7.4 %multiply_reduce_fusion.7 = f32[]{:T(128)} fusion(f32[48,1024]{1,0:T(8,128)S(1)} %get-tuple-element.222, f32[48,1024]{1,0:T(8,128)S(1)} %get-tuple-element.226, f32[]{:T(128)} %get-tuple-element.278, f32[1024]{0:T(1024)S(1)} %bitcast.125, f32[1024]{0:T(1024)S(1)} %bitcast.129, f32[1024]{0:T(1024)S(1)} %bitcast.121, f32[1024]{0:T(1024)S(1)} %bitcast.133, ...), kind=kOutput, calls=%fused_computation.6.clone.1.clone | convolution fusion | flops 622854144 | bytes 409616 | tf_op jit(solution)/shard_map/while/body/eval_jaxpr/dot_general | solution.py:38
  53.5 0.8 dynamic_update_slice.27
  54.3 4.2 %multiply_reduce_fusion.6 = f32[]{:T(128)} fusion(f32[]{:T(128)} %get-tuple-element.278, f32[1024]{0:T(1024)S(1)} %bitcast.126, f32[1024]{0:T(1024)S(1)} %bitcast.130, f32[1024]{0:T(1024)S(1)} %bitcast.122, f32[1024]{0:T(1024)S(1)} %bitcast.134, f32[]{:T(128)} %get-tuple-element.275, f32[]{:T(128)} %get-tuple-element.274), kind=kLoop, calls=%fused_computation.7.clone.1.clone | loop fusion | flops 15728639 | bytes 16400 | tf_op jit(solution)/shard_map/while/body/eval_jaxpr/reduce_sum | solution.py:78
  58.5 0.8 dynamic_update_slice.26
  60.7 3.2 %bitcast_dynamic-update-slice_fusion.6 = (f32[2,48,1024]{2,1,0:T(8,128)S(1)}, f32[48,1024]{1,0:T(8,128)S(1)}) fusion(f32[2,48,1024]{2,1,0:T(8,128)S(1)} %get-tuple-element.256, s32[]{:T(128)} %get-tuple-element.255, f32[]{:T(128)} %get-tuple-element.278, f32[1024]{0:T(1024)S(1)} %bitcast.123, f32[1024]{0:T(1024)S(1)} %bitcast.127, ...), kind=kOutput, calls=%fused_computation.12.clone.1.clone | convolution fusion | flops 115392512 | bytes 510976 | tf_op jit(solution)/shard_map/while/body/eval_jaxpr/dot_general | solution.py:29
  63.9 0.9 select_reduce_fusion.7
  66.9 4.4 %cholesky.73 = f32[48,48]{1,0:T(8,128)S(1)} custom-call(f32[48,48]{1,0:T(8,128)S(1)} %fusion.68), custom_call_target="Cholesky" | custom-call | tf_op jit(solution)/shard_map/while/body/eval_jaxpr/jit(cholesky)/cholesky | solution.py:36
  72.8 3.7 %custom-call.20 = f32[1,48,48]{1,2,0:T(8,128)S(1)} custom-call(f32[1,48,48]{2,1,0:T(8,128)S(1)} %fusion.69), custom_call_target="InvertDiagBlocksLowerTriangular" | custom-call | tf_op jit(solution)/shard_map/while/body/eval_jaxpr/jit(_cho_solve)/triangular_solve | solution.py:37
  76.4 3.2 %fusion.67 = f32[48,1024]{1,0:T(8,128)S(1)} fusion(f32[]{:T(128)} %get-tuple-element.278, f32[1024]{0:T(1024)S(1)} %bitcast.124, f32[1024]{0:T(1024)S(1)} %bitcast.128, f32[1024]{0:T(1024)S(1)} %bitcast.120, f32[1024]{0:T(1024)S(1)} %bitcast.132, f32[]{:T(128)} %get-tuple-element.275, f32[]{:T(128)} %get-tuple-element.274, ...), kind=kOutput, calls=%fused_computation.9.clone.1.clone | convolution fusion | flops 115392512 | bytes 409612 | tf_op jit(solution)/shard_map/while/body/eval_jaxpr/dot_general | solution.py:32
  80.3 7.4 %multiply_reduce_fusion.7 = f32[]{:T(128)} fusion(f32[48,1024]{1,0:T(8,128)S(1)} %get-tuple-element.222, f32[48,1024]{1,0:T(8,128)S(1)} %get-tuple-element.226, f32[]{:T(128)} %get-tuple-element.278, f32[1024]{0:T(1024)S(1)} %bitcast.125, f32[1024]{0:T(1024)S(1)} %bitcast.129, f32[1024]{0:T(1024)S(1)} %bitcast.121, f32[1024]{0:T(1024)S(1)} %bitcast.133, ...), kind=kOutput, calls=%fused_computation.6.clone.1.clone | convolution fusion | flops 622854144 | bytes 409616 | tf_op jit(solution)/shard_map/while/body/eval_jaxpr/dot_general | solution.py:38
  87.8 0.8 dynamic_update_slice.27
  88.6 4.2 %multiply_reduce_fusion.6 = f32[]{:T(128)} fusion(f32[]{:T(128)} %get-tuple-element.278, f32[1024]{0:T(1024)S(1)} %bitcast.126, f32[1024]{0:T(1024)S(1)} %bitcast.130, f32[1024]{0:T(1024)S(1)} %bitcast.122, f32[1024]{0:T(1024)S(1)} %bitcast.134, f32[]{:T(128)} %get-tuple-element.275, f32[]{:T(128)} %get-tuple-element.274), kind=kLoop, calls=%fused_computation.7.clone.1.clone | loop fusion | flops 15728639 | bytes 16400 | tf_op jit(solution)/shard_map/while/body/eval_jaxpr/reduce_sum | solution.py:78
  92.8 0.8 dynamic_update_slice.26
  94.2 39.7 %psum.14 = f32[]{:T(128)} all-reduce(f32[]{:T(128)} %fusion.22), channel_id=1, replica_groups=mesh['prow'=4,'pcol'=8] {'prow','pcol'}, use_global_device_ids=true, to_apply=%region_8.9 | all-reduce | flops 1 | bytes 8 | tf_op jit(solution)/shard_map/psum | solution.py:89
  135.1 1.0 select_bitcast_fusion
  136.8 41.0 %psum.15 = s32[1]{0:T(128)} all-reduce(s32[1]{0:T(128)} %bitcast.25), channel_id=1, replica_groups=mesh['prow'=4,'pcol'=8] {'prow','pcol'}, use_global_device_ids=true, to_apply=%region_10.11 | all-reduce | flops 1 | bytes 8 | tf_op jit(solution)/shard_map/psum | solution.py:68
  (43 shorter events, 12.3 us)
Async XLA Ops:
  0.6 23.7 %copy-start.1 = (s32[2,1,1,1]{0,3,2,1:T(1,128)S(1)}, s32[2,1,1,1]{0,3,2,1:T(1,128)}, u32[]{:S(2)}) copy-start(s32[2,1,1,1]{0,3,2,1:T(1,128)} %param.12) | copy-start | bytes 28
  24.4 0.7 copy-start
where the time goes:
time: 178 us
  blocking collectives  102 us (57%)
  other arithmetic  33.2 us (19%)
  matrix products  30.7 us (17%)
  local copies, waits for them, and re-layouts  6.5 us (4%)
  between operations  2.82 us (2%)
  loops' own time  2.75 us (2%)
    psum x1, blocking collectives, per_device(): rank_sum = lax.psum(ranks_local, ('prow', 'pcol'))  41 us
    psum x1, blocking collectives, per_device(): total = lax.psum(norm_local, ('prow', 'pcol'))  39.7 us
    dot_general x2, matrix products, compress(): lax.dot_general(sketched, coeffs, (((0,), (0,)), ((), ())), precision=lax...  14.9 us
    all_gather x1, blocking collectives, per_device(): gathered = lax.all_gather(points, 'pcol', axis=1, tiled=True)  10.9 us
    another operation x6, other arithmetic, compress(): factor = jnp.linalg.cholesky(gram)  10.3 us
    all_gather x1, blocking collectives, per_device(): bank_whole = lax.all_gather(sketch_bank, 'pcol', axis=0, tiled=True)  10.2 us
    another operation x4, other arithmetic, compress(): coeffs = jax.scipy.linalg.cho_solve((factor, True), product)  8.74 us
    reduce_sum x2, other arithmetic, one_tile(): norm_sq = jnp.sum(tile_block * tile_block)  8.47 us

commit v1 on v0

v1 whole, which is shorter than its diff:
```python
import functools
import math

import jax
import jax.numpy as jnp
from jax import lax
from jax.experimental import pallas as pl
from jax.experimental.pallas import tpu as pltpu
from jax.sharding import PartitionSpec as P

MESH = pl.DeviceIdType.MESH
LOG2E = math.log2(math.e)
F32 = jnp.float32
BF16 = jnp.bfloat16
HIGH = lax.Precision.HIGHEST


def dot(a, b, da, db, precision=None):
    return lax.dot_general(
        a, b, (((da,), (db,)), ((), ())), preferred_element_type=F32, precision=precision
    )


def split(x):
    high = x.astype(BF16)
    return high, (x - high.astype(F32)).astype(BF16)


def all_sum(x):
    return jnp.sum(jnp.sum(x, axis=1, keepdims=True), axis=0, keepdims=True)


def invert(mats):
    size = mats[0].shape[0]
    row_at = lax.broadcasted_iota(jnp.int32, (size, size), 0)
    col_at = lax.broadcasted_iota(jnp.int32, (size, size), 1)
    for k in range(size):
        following = []
        for m in mats:
            col = jnp.broadcast_to(m[:, k : k + 1], (size, size))
            inverse = 1.0 / col[k : k + 1, :]
            row = jnp.where(col_at[:1] == k, 1.0, m[k : k + 1, :]) * inverse
            rest = jnp.where(col_at == k, 0.0, m) - col * row
            following.append(jnp.where(row_at == k, row, rest))
        mats = following
    return mats


def kernel(
    rows,
    cols,
    row_tiles,
    col_tiles,
    points,
    range_length,
    smoothness,
    bank,
    ids,
    ranks,
    y_out,
    c_out,
    err_out,
    rank_out,
    all_points,
    all_bank,
    low,
    norms,
    residuals,
    mine,
    col_sums,
    partial,
    row_sums,
    sem_local,
    sem_ps,
    sem_pr,
    sem_bs,
    sem_br,
    sem_cs,
    sem_cr,
    sem_rs,
    sem_rr,
):
    p = lax.axis_index("prow")
    q = lax.axis_index("pcol")
    per_bank, sketch_rows, size = bank.shape
    across = cols * col_tiles
    slots = [(a, b) for a in range(row_tiles) for b in range(col_tiles)]
    sibling = q + 1 - 2 * lax.rem(q, 2)

    barrier = pltpu.get_barrier_semaphore()
    for step in range(1, cols):
        pl.semaphore_signal(
            barrier, device_id=(p, lax.rem(q + step, cols)), device_id_type=MESH
        )
    for step in range(1, rows):
        pl.semaphore_signal(
            barrier, device_id=(lax.rem(p + step, rows), q), device_id_type=MESH
        )
    own_points = pltpu.make_async_copy(points.at[:, 0], all_points.at[q], sem_local.at[0])
    own_bank = pltpu.make_async_copy(
        bank, all_bank.at[pl.ds(q * per_bank, per_bank)], sem_local.at[1]
    )
    own_points.start()
    own_bank.start()
    pl.semaphore_wait(barrier, cols + rows - 2)

    def point_copy(source, target):
        return pltpu.make_async_remote_copy(
            src_ref=points.at[:, 0],
            dst_ref=all_points.at[source],
            send_sem=sem_ps.at[target],
            recv_sem=sem_pr.at[source],
            device_id=(p, target),
            device_id_type=MESH,
        )

    def bank_copy(block, target, send):
        return pltpu.make_async_remote_copy(
            src_ref=all_bank.at[pl.ds(block * per_bank, per_bank)] if send >= cols else bank,
            dst_ref=all_bank.at[pl.ds(block * per_bank, per_bank)],
            send_sem=sem_bs.at[send],
            recv_sem=sem_br.at[block],
            device_id=(p, target),
            device_id_type=MESH,
        )

    for step in range(1, cols):
        point_copy(q, lax.rem(q + step, cols)).start()
    for step in range(2, cols, 2):
        bank_copy(q, lax.rem(q + step, cols), step).start()
    bank_copy(q, sibling, 1).start()

    degree = jnp.full((8, 128), smoothness[0].astype(F32))
    scale = (LOG2E * jnp.sqrt(2.0 * degree + 1.0)) / jnp.full((8, 128), range_length[0])
    scale = scale[:1]
    linear = jnp.where(smoothness[0] >= 1, 1.0 / LOG2E, 0.0).astype(F32)
    square = jnp.where(smoothness[0] >= 2, 1.0 / (3.0 * LOG2E * LOG2E), 0.0).astype(F32)

    own_points.wait()
    for step in range(1, cols):
        point_copy(lax.rem(q + step, cols), q).wait_recv()

    def place(slot):
        a, b = slots[slot]
        return a * rows + p, b * cols + q

    def generate(slot):
        i, j = place(slot)

        @pl.when(j > i)
        def _():
            norms[slot] = jnp.zeros((8, 128), F32)

        @pl.when(j <= i)
        def _():
            row_block = lax.rem(i, cols)
            row_major = i // cols
            col_major = slots[slot][1]

            def chunk(c, total):
                at = pl.ds(pl.multiple_of(c * 128, 128), 128)
                x_row = all_points[row_block, row_major, 0:1, at] * scale
                y_row = all_points[row_block, row_major, 1:2, at] * scale
                x_row = jnp.broadcast_to(x_row, (128, 128)).T
                y_row = jnp.broadcast_to(y_row, (128, 128)).T
                for n in range(size // 128):
                    cut = slice(n * 128, n * 128 + 128)
                    x_col = points[col_major, 0, 0:1, cut] * scale
                    y_col = points[col_major, 0, 1:2, cut] * scale
                    dx = x_row - x_col
                    dy = y_row - y_col
                    d2 = dx * dx + dy * dy
                    t = d2 * lax.rsqrt(jnp.maximum(d2, 1e-30))
                    tile = (1.0 + linear * t + square * d2) * jnp.exp2(-t)
                    low[slot, at, cut] = tile.astype(BF16)
                    total = total + jnp.sum((tile * tile).reshape(16, 8, 128), axis=0)
                return total

            norms[slot] = lax.fori_loop(0, size // 128, chunk, jnp.zeros((8, 128), F32))

    generate(0)
    for step in range(2, cols, 2):
        block = lax.rem(q + step, cols)
        bank_copy(block, q, 0).wait_recv()
        bank_copy(block, sibling, cols + step).start()
    for slot in range(1, len(slots)):
        generate(slot)

    norm_sum = jnp.zeros((1, 1), F32)
    rank_sum = jnp.float32(0)
    for slot, (a, b) in enumerate(slots):
        i, j = place(slot)
        weight = jnp.where(j < i, 2.0, 1.0).astype(F32)
        norm_sum = norm_sum + weight * all_sum(norms[slot])
        rank_sum = rank_sum + jnp.where(j < i, ranks[a, 0, b, 0], 0).astype(F32)
    first = lax.broadcasted_iota(jnp.int32, (8, 128), 0) == 0
    mine[...] = jnp.where(first, jnp.broadcast_to(norm_sum, (8, 128)), rank_sum)

    own_bank.wait()
    bank_copy(sibling, q, 0).wait_recv()
    for step in range(2, cols, 2):
        bank_copy(lax.rem(sibling + step, cols), q, 0).wait_recv()

    def keep_of(a, b):
        return lax.broadcasted_iota(jnp.int32, (sketch_rows, 1), 0) < ranks[a, 0, b, 0]

    for slot, (a, b) in enumerate(slots):
        i, j = place(slot)

        @pl.when(j < i)
        def _():
            sketch = all_bank[ids[a, 0, b, 0]]
            sketch = jnp.where(keep_of(a, b), sketch.astype(F32), 0.0).astype(BF16)
            y_out[a, 0, b, 0] = dot(sketch, low[slot], 1, 1)

        @pl.when(j >= i)
        def _():
            y_out[a, 0, b, 0] = jnp.zeros((sketch_rows, size), F32)
            c_out[a, 0, b, 0] = jnp.zeros((sketch_rows, size), F32)
            residuals[slot] = norms[slot]

    def row_copy(source, target):
        return pltpu.make_async_remote_copy(
            src_ref=mine,
            dst_ref=row_sums.at[source],
            send_sem=sem_rs.at[target],
            recv_sem=sem_rr.at[source],
            device_id=(target, q),
            device_id_type=MESH,
        )

    def col_copy(source, target):
        return pltpu.make_async_remote_copy(
            src_ref=partial,
            dst_ref=col_sums.at[source],
            send_sem=sem_cs.at[target],
            recv_sem=sem_cr.at[source],
            device_id=(p, target),
            device_id_type=MESH,
        )

    for step in range(1, rows):
        row_copy(p, lax.rem(p + step, rows)).start()

    eye = lax.broadcasted_iota(jnp.int32, (sketch_rows, sketch_rows), 0) == (
        lax.broadcasted_iota(jnp.int32, (sketch_rows, sketch_rows), 1)
    )
    grams = []
    for slot, (a, b) in enumerate(slots):
        i, j = place(slot)
        y = y_out[a, 0, b, 0]
        gram = dot(y, y, 1, 1, HIGH)
        rank = jnp.full((1, 1), ranks[a, 0, b, 0].astype(F32))
        shift = 0.1 * all_sum(jnp.where(eye, gram, 0.0)) / rank
        diagonal = jnp.where(keep_of(a, b) & (j < i), shift, 1.0)
        grams.append(gram + jnp.where(eye, diagonal, 0.0))
    inverses = invert(grams)

    summed = mine[...]
    for step in range(1, rows):
        source = lax.rem(p + step, rows)
        row_copy(source, p).wait_recv()
        summed = summed + row_sums[source]
    partial[...] = summed

    for slot, (a, b) in enumerate(slots):
        i, j = place(slot)

        @pl.when(j < i)
        def _():
            product = dot(y_out[a, 0, b, 0].astype(BF16), low[slot], 1, 0)
            c_out[a, 0, b, 0] = dot(inverses[slot], product, 1, 0, HIGH)

    for step in range(1, cols):
        col_copy(q, lax.rem(q + step, cols)).start()

    for slot, (a, b) in enumerate(slots):
        i, j = place(slot)

        @pl.when(j < i)
        def _():
            y_high, y_low = split(y_out[a, 0, b, 0])
            c_high, c_low = split(c_out[a, 0, b, 0])
            left = jnp.concatenate([y_high, y_high, y_low], axis=0)
            right = jnp.concatenate([c_high, c_low, c_high], axis=0)
            total = jnp.zeros((8, 128), F32)
            for m in range(size // 128):
                cut = slice(m * 128, m * 128 + 128)
                gap = low[slot, cut].astype(F32) - dot(left[:, cut], right, 0, 0)
                gap = gap * gap
                for n in range(size // 128):
                    total = total + jnp.sum(
                        gap[:, n * 128 : n * 128 + 128].reshape(16, 8, 128), axis=0
                    )
            residuals[slot] = total

    whole = partial[...]
    for step in range(1, cols):
        source = lax.rem(q + step, cols)
        col_copy(source, q).wait_recv()
        whole = whole + col_sums[source]
    total = whole[0:1, 0:1]
    for slot, (a, b) in enumerate(slots):
        i, j = place(slot)
        error = jnp.sqrt(all_sum(residuals[slot])) * float(across) / jnp.sqrt(total)
        err_out[a, 0, b, 0] = jnp.where(j <= i, error, 0.0)[0, 0]
    rank_out[0] = whole[1:2, 0:1].astype(jnp.int32)[0, 0]

    for step in range(1, cols):
        target = lax.rem(q + step, cols)
        point_copy(q, target).wait_send()
        col_copy(q, target).wait_send()
    for step in range(2, cols, 2):
        bank_copy(q, lax.rem(q + step, cols), step).wait_send()
        bank_copy(lax.rem(q + step, cols), sibling, cols + step).wait_send()
    bank_copy(q, sibling, 1).wait_send()
    for step in range(1, rows):
        row_copy(p, lax.rem(p + step, rows)).wait_send()


def per_device(rows, cols, points, range_length, smoothness, bank, ids, ranks):
    row_tiles, col_tiles = ids.shape[0], ids.shape[2]
    per_bank, sketch_rows, size = bank.shape
    slots = row_tiles * col_tiles
    factors = jax.ShapeDtypeStruct((row_tiles, 1, col_tiles, 1, sketch_rows, size), F32)
    vmem = pl.BlockSpec(memory_space=pltpu.VMEM)
    smem = pl.BlockSpec(memory_space=pltpu.SMEM)
    dma = pltpu.SemaphoreType.DMA
    return pl.pallas_call(
        functools.partial(kernel, rows, cols, row_tiles, col_tiles),
        out_shape=(
            factors,
            factors,
            jax.ShapeDtypeStruct((row_tiles, 1, col_tiles, 1), F32),
            jax.ShapeDtypeStruct((1,), jnp.int32),
        ),
        in_specs=[vmem, smem, smem, vmem, smem, smem],
        out_specs=(vmem, vmem, smem, smem),
        scratch_shapes=[
            pltpu.VMEM((cols, col_tiles, 2, size), F32),
            pltpu.VMEM((cols * per_bank, sketch_rows, size), BF16),
            pltpu.VMEM((slots, size, size), BF16),
            pltpu.VMEM((slots, 8, 128), F32),
            pltpu.VMEM((slots, 8, 128), F32),
            pltpu.VMEM((8, 128), F32),
            pltpu.VMEM((cols, 8, 128), F32),
            pltpu.VMEM((8, 128), F32),
            pltpu.VMEM((rows, 8, 128), F32),
            dma((2,)),
            dma((cols,)),
            dma((cols,)),
            dma((2 * cols,)),
            dma((cols,)),
            dma((cols,)),
            dma((cols,)),
            dma((rows,)),
            dma((rows,)),
        ],
        compiler_params=pltpu.CompilerParams(
            collective_id=0, has_side_effects=True, vmem_limit_bytes=48 * 1024 * 1024
        ),
        name="tiles",
    )(points, range_length, smoothness, bank, ids, ranks)


def solution(mesh):
    in_specs = (
        P(None, "pcol", None, None),
        P(),
        P(),
        P("pcol", None, None),
        P(None, "prow", None, "pcol"),
        P(None, "prow", None, "pcol"),
    )
    out_specs = (
        P(None, "prow", None, "pcol", None, None),
        P(None, "prow", None, "pcol", None, None),
        P(None, "prow", None, "pcol"),
        P(),
    )
    return jax.shard_map(
        functools.partial(per_device, mesh.shape["prow"], mesh.shape["pcol"]),
        mesh=mesh,
        in_specs=in_specs,
        out_specs=out_specs,
        check_vma=False,
    )
```

time: 178 us -> 34.7 us (0.19)
  blocking collectives: 102 us -> 0 us
  other arithmetic: 33.2 us -> 0 us
  matrix products: 30.7 us -> 0 us
  Pallas kernels: 0 us -> 26.3 us
  loops' own time: 2.75 us -> 0 us
  local copies, waits for them, and re-layouts: 6.5 us -> 4.42 us
    psum x2 -> x0, blocking collectives: 80.7 us -> none  [the longest x1 41 us: per_device(): rank_sum = lax.psum(ranks_local, ('prow', 'pcol'))]
    dot_general x8 -> x0, matrix products: 29.3 us -> none  [the longest x2 14.9 us: compress(): lax.dot_general(sketched, coeffs, (((0,), (0,)), ((), ())), precision=lax...]
    pallas_call x0 -> x1, Pallas kernels: none -> 26.3 us  [per_device(): pl.pallas_call(functools.partial(kernel, rows, cols, row_tiles, col_tiles...]
    all_gather x2 -> x0, blocking collectives: 21.1 us -> none  [the longest x1 10.9 us: per_device(): gathered = lax.all_gather(points, 'pcol', axis=1, tiled=True)]
    another operation x12 -> x0, other arithmetic: 19 us -> none  [the longest x6 10.3 us: compress(): factor = jnp.linalg.cholesky(gram)]
    reduce_sum x4 -> x0, other arithmetic: 9.71 us -> none  [the longest x2 8.47 us: one_tile(): norm_sq = jnp.sum(tile_block * tile_block)]
    unnamed x4 -> x12, local copies, waits for them, and re-layouts: 0.01 us -> 3.82 us
    dynamic_update_slice x4 -> x0, local copies, waits for them, and re-layouts: 3.2 us -> none  [per_device(): lax.map(mapped, (row_points_all, col_points_all, chosen, own_ranks))]
where the time goes in v1:
time: 34.7 us; the launch traced here: 34.4 us
  Pallas kernels  26.3 us (76%)
  local copies, waits for them, and re-layouts  4.42 us (13%)
  between operations  3.72 us (11%)
    pallas_call x1, Pallas kernels, per_device(): pl.pallas_call(functools.partial(kernel, rows, cols, row_tiles, col_tiles...  26.3 us
    unnamed x12, local copies, waits for them, and re-layouts  3.82 us

profile of v1, /device:TPU:0, one launch (start us, length us, event | category | flops | bytes accessed | tf_op | source)
XLA Modules:
  0.0 34.4 jit_solution(2427476725958108242)
XLA Ops:
  1.3 0.0 copy-start.2
  1.9 0.0 copy-done.2
  2.0 0.0 copy-start.3
  2.0 0.1 copy.10.ids
  2.1 0.6 %copy-done.3 = s32[2,1,1,1]{0,3,2,1:T(1,128)S(1)} copy-done((s32[2,1,1,1]{0,3,2,1:T(1,128)S(1)}, s32[2,1,1,1]{0,3,2,1:T(1,128)}, u32[]{:S(2)}) %copy-start.3) | copy-done | bytes 32
  2.6 0.1 copy.11.ranks
  2.7 0.0 copy-start
  2.7 0.9 %copy-done = bf16[1,48,1024]{2,1,0:T(8,128)(2,1)S(1)} copy-done((bf16[1,48,1024]{2,1,0:T(8,128)(2,1)S(1)}, bf16[1,48,1024]{2,1,0:T(8,128)(2,1)}, u32[]{:S(2)}) %copy-start) | copy-done | bytes 98328
  3.6 0.0 copy-start.1
  3.6 0.7 %copy-done.1 = f32[1,1,2,1024]{3,2,1,0:T(2,128)S(1)} copy-done((f32[1,1,2,1024]{3,2,1,0:T(2,128)S(1)}, f32[1,1,2,1024]{3,2,1,0:T(2,128)}, u32[]{:S(2)}) %copy-start.1) | copy-done | bytes 8216
  4.3 26.3 %tiles.1 = (f32[2,1,1,1,48,1024]{5,4,3,2,1,0:T(8,128)S(1)}, f32[2,1,1,1,48,1024]{5,4,3,2,1,0:T(8,128)S(1)}, f32[2,1,1,1]{3,2,1,0:T(1,128)S(1)}, s32[1]{0:T(128)}) custom-call(f32[1,1,2,1024]{3,2,1,0:T(2,128)S(1)} %copy-done.1, f32[1]{0:T(128)S(6)} %copy.16.range_length, s32[1]{0:T(128)S(6)} %copy.17.smoothness, bf16[1,48,1024]{2,1,0:T(8,128)(2,1)S(1)} %copy-done, ...), custom_call_target="tpu_custom_call" | custom-call | tf_op jit(solution)/shard_map/tiles/pallas_call | solution.py:329
  30.6 0.6 %copy.12 = f32[2,1,1,1]{0,3,2,1:T(1,128)} copy(f32[2,1,1,1]{3,2,1,0:T(1,128)S(1)} %get-tuple-element.6) | data formatting | bytes 16 | tf_op jit(solution)/shard_map/tiles/pallas_call | solution.py:329
  31.2 0.7 %copy.18 = f32[2,1,1,1,48,1024]{5,4,3,2,1,0:T(8,128)} copy(f32[2,1,1,1,48,1024]{5,4,3,2,1,0:T(8,128)S(1)} %get-tuple-element.12) | data formatting | bytes 786432
  32.0 0.7 %copy.19 = f32[2,1,1,1,48,1024]{5,4,3,2,1,0:T(8,128)} copy(f32[2,1,1,1,48,1024]{5,4,3,2,1,0:T(8,128)S(1)} %get-tuple-element.13) | data formatting | bytes 786432
Async XLA Ops:
  1.3 0.7 %copy-start.2 = (s32[2,1,1,1]{0,3,2,1:T(1,128)S(1)}, s32[2,1,1,1]{0,3,2,1:T(1,128)}, u32[]{:S(2)}) copy-start(s32[2,1,1,1]{0,3,2,1:T(1,128)} %param.10) | copy-start | bytes 28
  2.0 0.7 %copy-start.3 = (s32[2,1,1,1]{0,3,2,1:T(1,128)S(1)}, s32[2,1,1,1]{0,3,2,1:T(1,128)}, u32[]{:S(2)}) copy-start(s32[2,1,1,1]{0,3,2,1:T(1,128)} %param.11) | copy-start | bytes 28
  2.7 0.9 %copy-start = (bf16[1,48,1024]{2,1,0:T(8,128)(2,1)S(1)}, bf16[1,48,1024]{2,1,0:T(8,128)(2,1)}, u32[]{:S(2)}) copy-start(bf16[1,48,1024]{2,1,0:T(8,128)(2,1)} %bank.1) | copy-start | bytes 294916
  3.6 0.7 %copy-start.1 = (f32[1,1,2,1024]{3,2,1,0:T(2,128)S(1)}, f32[1,1,2,1024]{3,2,1,0:T(2,128)}, u32[]{:S(2)}) copy-start(f32[1,1,2,1024]{3,2,1,0:T(2,128)} %points.1) | copy-start | bytes 24580

commit v2 on v1

--- a/solution.py
+++ b/solution.py
@@ -51,21 +51,23 @@
     cols,
     row_tiles,
     col_tiles,
-    points,
     range_length,
     smoothness,
-    bank,
+    points_hbm,
+    bank_hbm,
+    ids_hbm,
+    ranks_hbm,
+    y_out,
+    c_out,
+    residuals,
+    whole_out,
+    points,
     ids,
     ranks,
-    y_out,
-    c_out,
-    err_out,
-    rank_out,
     all_points,
     all_bank,
     low,
     norms,
-    residuals,
     mine,
     col_sums,
     partial,
@@ -82,8 +84,7 @@
 ):
     p = lax.axis_index("prow")
     q = lax.axis_index("pcol")
-    per_bank, sketch_rows, size = bank.shape
-    across = cols * col_tiles
+    per_bank, sketch_rows, size = bank_hbm.shape
     slots = [(a, b) for a in range(row_tiles) for b in range(col_tiles)]
     sibling = q + 1 - 2 * lax.rem(q, 2)
 
@@ -96,17 +97,28 @@
         pl.semaphore_signal(
             barrier, device_id=(lax.rem(p + step, rows), q), device_id_type=MESH
         )
-    own_points = pltpu.make_async_copy(points.at[:, 0], all_points.at[q], sem_local.at[0])
-    own_bank = pltpu.make_async_copy(
-        bank, all_bank.at[pl.ds(q * per_bank, per_bank)], sem_local.at[1]
-    )
-    own_points.start()
-    own_bank.start()
+    local = [
+        pltpu.make_async_copy(source, target, sem_local.at[index])
+        for index, (source, target) in enumerate(
+            [
+                (points_hbm, points),
+                (ids_hbm, ids),
+                (ranks_hbm, ranks),
+                (points_hbm.at[:, 0], all_points.at[q]),
+                (bank_hbm, all_bank.at[pl.ds(q * per_bank, per_bank)]),
+            ]
+        )
+    ]
+    for copy in local:
+        copy.start()
+    needed = q < 0
+    for a in range(row_tiles):
+        needed = needed | (lax.rem(a * rows + p, cols) == q)
     pl.semaphore_wait(barrier, cols + rows - 2)
 
     def point_copy(source, target):
         return pltpu.make_async_remote_copy(
-            src_ref=points.at[:, 0],
+            src_ref=points_hbm.at[:, 0],
             dst_ref=all_points.at[source],
             send_sem=sem_ps.at[target],
             recv_sem=sem_pr.at[source],
@@ -116,7 +128,7 @@
 
     def bank_copy(block, target, send):
         return pltpu.make_async_remote_copy(
-            src_ref=all_bank.at[pl.ds(block * per_bank, per_bank)] if send >= cols else bank,
+            src_ref=all_bank.at[pl.ds(block * per_bank, per_bank)] if send >= cols else bank_hbm,
             dst_ref=all_bank.at[pl.ds(block * per_bank, per_bank)],
             send_sem=sem_bs.at[send],
             recv_sem=sem_br.at[block],
@@ -124,28 +136,43 @@
             device_id_type=MESH,
         )
 
-    for step in range(1, cols):
-        point_copy(q, lax.rem(q + step, cols)).start()
+    @pl.when(needed)
+    def _():
+        for step in range(1, cols):
+            point_copy(q, lax.rem(q + step, cols)).start()
+
     for step in range(2, cols, 2):
         bank_copy(q, lax.rem(q + step, cols), step).start()
     bank_copy(q, sibling, 1).start()
 
+    for copy in local[:-1]:
+        copy.wait()
     degree = jnp.full((8, 128), smoothness[0].astype(F32))
     scale = (LOG2E * jnp.sqrt(2.0 * degree + 1.0)) / jnp.full((8, 128), range_length[0])
     scale = scale[:1]
     linear = jnp.where(smoothness[0] >= 1, 1.0 / LOG2E, 0.0).astype(F32)
     square = jnp.where(smoothness[0] >= 2, 1.0 / (3.0 * LOG2E * LOG2E), 0.0).astype(F32)
 
-    own_points.wait()
-    for step in range(1, cols):
-        point_copy(lax.rem(q + step, cols), q).wait_recv()
-
     def place(slot):
         a, b = slots[slot]
         return a * rows + p, b * cols + q
 
+    arrived = []
+
     def generate(slot):
         i, j = place(slot)
+        a = slots[slot][0]
+        owner = lax.rem(a * rows + p, cols)
+        fresh = owner != q
+        for before in arrived:
+            if before != a:
+                fresh = fresh & (owner != lax.rem(before * rows + p, cols))
+        if a not in arrived:
+            arrived.append(a)
+
+            @pl.when(fresh)
+            def _():
+                point_copy(owner, q).wait_recv()
 
         @pl.when(j > i)
         def _():
@@ -186,39 +213,6 @@
     for slot in range(1, len(slots)):
         generate(slot)
 
-    norm_sum = jnp.zeros((1, 1), F32)
-    rank_sum = jnp.float32(0)
-    for slot, (a, b) in enumerate(slots):
-        i, j = place(slot)
-        weight = jnp.where(j < i, 2.0, 1.0).astype(F32)
-        norm_sum = norm_sum + weight * all_sum(norms[slot])
-        rank_sum = rank_sum + jnp.where(j < i, ranks[a, 0, b, 0], 0).astype(F32)
-    first = lax.broadcasted_iota(jnp.int32, (8, 128), 0) == 0
-    mine[...] = jnp.where(first, jnp.broadcast_to(norm_sum, (8, 128)), rank_sum)
-
-    own_bank.wait()
-    bank_copy(sibling, q, 0).wait_recv()
-    for step in range(2, cols, 2):
-        bank_copy(lax.rem(sibling + step, cols), q, 0).wait_recv()
-
-    def keep_of(a, b):
-        return lax.broadcasted_iota(jnp.int32, (sketch_rows, 1), 0) < ranks[a, 0, b, 0]
-
-    for slot, (a, b) in enumerate(slots):
-        i, j = place(slot)
-
-        @pl.when(j < i)
-        def _():
-            sketch = all_bank[ids[a, 0, b, 0]]
-            sketch = jnp.where(keep_of(a, b), sketch.astype(F32), 0.0).astype(BF16)
-            y_out[a, 0, b, 0] = dot(sketch, low[slot], 1, 1)
-
-        @pl.when(j >= i)
-        def _():
-            y_out[a, 0, b, 0] = jnp.zeros((sketch_rows, size), F32)
-            c_out[a, 0, b, 0] = jnp.zeros((sketch_rows, size), F32)
-            residuals[slot] = norms[slot]
-
     def row_copy(source, target):
         return pltpu.make_async_remote_copy(
             src_ref=mine,
@@ -239,8 +233,41 @@
             device_id_type=MESH,
         )
 
-    for step in range(1, rows):
-        row_copy(p, lax.rem(p + step, rows)).start()
+    norm_sum = jnp.zeros((1, 1), F32)
+    rank_sum = jnp.float32(0)
+    for slot, (a, b) in enumerate(slots):
+        i, j = place(slot)
+        weight = jnp.where(j < i, 2.0, 1.0).astype(F32)
+        norm_sum = norm_sum + weight * all_sum(norms[slot])
+        rank_sum = rank_sum + jnp.where(j < i, ranks[0, b, 0, a], 0).astype(F32)
+    first = lax.broadcasted_iota(jnp.int32, (8, 128), 0) == 0
+    mine[...] = jnp.where(first, jnp.broadcast_to(norm_sum, (8, 128)), rank_sum)
+
+    local[-1].wait()
+    bank_copy(sibling, q, 0).wait_recv()
+    for step in range(2, cols, 2):
+        bank_copy(lax.rem(sibling + step, cols), q, 0).wait_recv()
+
+    def keep_of(a, b):
+        return lax.broadcasted_iota(jnp.int32, (sketch_rows, 1), 0) < ranks[0, b, 0, a]
+
+    for slot, (a, b) in enumerate(slots):
+        i, j = place(slot)
+        if slot == 0:
+            for step in range(1, rows):
+                row_copy(p, lax.rem(p + step, rows)).start()
+
+        @pl.when(j < i)
+        def _():
+            sketch = all_bank[ids[0, b, 0, a]]
+            sketch = jnp.where(keep_of(a, b), sketch.astype(F32), 0.0).astype(BF16)
+            y_out[a, 0, b, 0] = dot(sketch, low[slot], 1, 1)
+
+        @pl.when(j >= i)
+        def _():
+            y_out[a, 0, b, 0] = jnp.zeros((sketch_rows, size), F32)
+            c_out[a, 0, b, 0] = jnp.zeros((sketch_rows, size), F32)
+            residuals[slot] = norms[slot]
 
     eye = lax.broadcasted_iota(jnp.int32, (sketch_rows, sketch_rows), 0) == (
         lax.broadcasted_iota(jnp.int32, (sketch_rows, sketch_rows), 1)
@@ -250,7 +277,7 @@
         i, j = place(slot)
         y = y_out[a, 0, b, 0]
         gram = dot(y, y, 1, 1, HIGH)
-        rank = jnp.full((1, 1), ranks[a, 0, b, 0].astype(F32))
+        rank = jnp.full((1, 1), ranks[0, b, 0, a].astype(F32))
         shift = 0.1 * all_sum(jnp.where(eye, gram, 0.0)) / rank
         diagonal = jnp.where(keep_of(a, b) & (j < i), shift, 1.0)
         grams.append(gram + jnp.where(eye, diagonal, 0.0))
@@ -299,17 +326,16 @@
         source = lax.rem(q + step, cols)
         col_copy(source, q).wait_recv()
         whole = whole + col_sums[source]
-    total = whole[0:1, 0:1]
-    for slot, (a, b) in enumerate(slots):
-        i, j = place(slot)
-        error = jnp.sqrt(all_sum(residuals[slot])) * float(across) / jnp.sqrt(total)
-        err_out[a, 0, b, 0] = jnp.where(j <= i, error, 0.0)[0, 0]
-    rank_out[0] = whole[1:2, 0:1].astype(jnp.int32)[0, 0]
+    whole_out[...] = whole
 
     for step in range(1, cols):
-        target = lax.rem(q + step, cols)
-        point_copy(q, target).wait_send()
-        col_copy(q, target).wait_send()
+        col_copy(q, lax.rem(q + step, cols)).wait_send()
+
+    @pl.when(needed)
+    def _():
+        for step in range(1, cols):
+            point_copy(q, lax.rem(q + step, cols)).wait_send()
+
     for step in range(2, cols, 2):
         bank_copy(q, lax.rem(q + step, cols), step).wait_send()
         bank_copy(lax.rem(q + step, cols), sibling, cols + step).wait_send()
@@ -318,35 +344,64 @@
         row_copy(p, lax.rem(p + step, rows)).wait_send()
 
 
+def finish(rows, cols, row_tiles, col_tiles, y, c, residuals, whole, y_out, c_out, err_out, rank_out, sems):
+    p = lax.axis_index("prow")
+    q = lax.axis_index("pcol")
+    copies = [
+        pltpu.make_async_copy(y, y_out, sems.at[0]),
+        pltpu.make_async_copy(c, c_out, sems.at[1]),
+    ]
+    for copy in copies:
+        copy.start()
+    norm = lax.rsqrt(whole[0:1, :]) * float(cols * col_tiles)
+    lane = lax.broadcasted_iota(jnp.int32, (1, 128), 1)
+    for b in range(col_tiles):
+        line = jnp.zeros((1, 128), F32)
+        for a in range(row_tiles):
+            error = jnp.sqrt(all_sum(residuals[a * col_tiles + b])) * norm
+            shown = (lane == a) & (b * cols + q <= a * rows + p)
+            line = jnp.where(shown, error, line)
+        err_out[0, b, 0:1, :] = line[:, :row_tiles]
+    rank_out[0] = whole[1:2, 0:1].astype(jnp.int32)[0, 0]
+    for copy in copies:
+        copy.wait()
+
+
 def per_device(rows, cols, points, range_length, smoothness, bank, ids, ranks):
     row_tiles, col_tiles = ids.shape[0], ids.shape[2]
     per_bank, sketch_rows, size = bank.shape
     slots = row_tiles * col_tiles
+    ids = ids.transpose(1, 2, 3, 0)
+    ranks = ranks.transpose(1, 2, 3, 0)
     factors = jax.ShapeDtypeStruct((row_tiles, 1, col_tiles, 1, sketch_rows, size), F32)
     vmem = pl.BlockSpec(memory_space=pltpu.VMEM)
     smem = pl.BlockSpec(memory_space=pltpu.SMEM)
+    hbm = pl.BlockSpec(memory_space=pltpu.HBM)
     dma = pltpu.SemaphoreType.DMA
-    return pl.pallas_call(
+    pinned = [pltpu.with_memory_space_constraint(x, pltpu.HBM) for x in (points, bank, ids, ranks)]
+    y, c, residuals, whole = pl.pallas_call(
         functools.partial(kernel, rows, cols, row_tiles, col_tiles),
         out_shape=(
             factors,
             factors,
-            jax.ShapeDtypeStruct((row_tiles, 1, col_tiles, 1), F32),
-            jax.ShapeDtypeStruct((1,), jnp.int32),
+            jax.ShapeDtypeStruct((slots, 8, 128), F32),
+            jax.ShapeDtypeStruct((8, 128), F32),
         ),
-        in_specs=[vmem, smem, smem, vmem, smem, smem],
-        out_specs=(vmem, vmem, smem, smem),
+        in_specs=[smem, smem, hbm, hbm, hbm, hbm],
+        out_specs=(vmem,) * 4,
         scratch_shapes=[
+            pltpu.VMEM(points.shape, F32),
+            pltpu.SMEM(ids.shape, jnp.int32),
+            pltpu.SMEM(ranks.shape, jnp.int32),
             pltpu.VMEM((cols, col_tiles, 2, size), F32),
             pltpu.VMEM((cols * per_bank, sketch_rows, size), BF16),
             pltpu.VMEM((slots, size, size), BF16),
-            pltpu.VMEM((slots, 8, 128), F32),
             pltpu.VMEM((slots, 8, 128), F32),
             pltpu.VMEM((8, 128), F32),
             pltpu.VMEM((cols, 8, 128), F32),
             pltpu.VMEM((8, 128), F32),
             pltpu.VMEM((rows, 8, 128), F32),
-            dma((2,)),
+            dma((5,)),
             dma((cols,)),
             dma((cols,)),
             dma((2 * cols,)),
@@ -357,10 +412,25 @@
             dma((rows,)),
         ],
         compiler_params=pltpu.CompilerParams(
-            collective_id=0, has_side_effects=True, vmem_limit_bytes=48 * 1024 * 1024
+            collective_id=0, has_side_effects=True, vmem_limit_bytes=40 * 1024 * 1024
         ),
         name="tiles",
-    )(points, range_length, smoothness, bank, ids, ranks)
+    )(range_length, smoothness, *pinned)
+    y, c, errors, rank_total = pl.pallas_call(
+        functools.partial(finish, rows, cols, row_tiles, col_tiles),
+        out_shape=(
+            factors,
+            factors,
+            jax.ShapeDtypeStruct((1, col_tiles, 1, row_tiles), F32),
+            jax.ShapeDtypeStruct((1,), jnp.int32),
+        ),
+        in_specs=[vmem] * 4,
+        out_specs=(hbm, hbm, vmem, smem),
+        scratch_shapes=[dma((2,))],
+        compiler_params=pltpu.CompilerParams(vmem_limit_bytes=16 * 1024 * 1024),
+        name="finish",
+    )(y, c, residuals, whole)
+    return y, c, errors.transpose(3, 0, 1, 2), rank_total
 
 
 def solution(mesh):

time: 34.7 us -> 28.4 us (0.82)
  local copies, waits for them, and re-layouts: 4.42 us -> 0 us
  between operations: 3.72 us -> 1.93 us
    unnamed x12 -> x0, local copies, waits for them, and re-layouts: 3.82 us -> none
    pallas_call x0 -> x1, Pallas kernels: none -> 1.41 us  [per_device(): pl.pallas_call(functools.partial(finish, rows, cols, row_tiles, col_tiles...]
    pallas_call x1, Pallas kernels: 26.3 us -> 24.9 us  [per_device(): pl.pallas_call(functools.partial(kernel, rows, cols, row_tiles, col_tiles...]
    pallas_call x1 -> x0, local copies, waits for them, and re-layouts: 0.6 us -> none  [per_device(): pl.pallas_call(functools.partial(kernel, rows, cols, row_tiles, col_tiles...]
where the time goes in v2:
time: 28.4 us; the launch traced here: 28.3 us
  Pallas kernels  26.3 us (93%)
  between operations  1.93 us (7%)
    pallas_call x1, Pallas kernels, per_device(): pl.pallas_call(functools.partial(kernel, rows, cols, row_tiles, col_tiles...  24.9 us
    pallas_call x1, Pallas kernels, per_device(): pl.pallas_call(functools.partial(finish, rows, cols, row_tiles, col_tiles...  1.41 us

profile of v2, /device:TPU:0, one launch (start us, length us, event | category | flops | bytes accessed | tf_op | source)
XLA Modules:
  0.0 28.3 jit_solution(17959397334088487127)
XLA Ops:
  1.9 24.9 %tiles.1 = (f32[2,1,1,1,48,1024]{5,4,3,2,1,0:T(8,128)S(1)}, f32[2,1,1,1,48,1024]{5,4,3,2,1,0:T(8,128)S(1)}, f32[2,8,128]{2,1,0:T(8,128)S(1)}, f32[8,128]{1,0:T(8,128)S(1)}) custom-call(f32[1]{0:T(128)S(6)} %copy.10.range_length, s32[1]{0:T(128)S(6)} %copy.11.smoothness, f32[1,1,2,1024]{3,2,1,0:T(2,128)} %points_hbm.1, bf16[1,48,1024]{2,1,0:T(8,128)(2,1)} %bank_hbm.1, ...), custom_call_target="tpu_custom_call" | custom-call | tf_op jit(solution)/shard_map/tiles/pallas_call | solution.py:382
  26.8 1.4 %finish.1 = (f32[2,1,1,1,48,1024]{5,4,3,2,1,0:T(8,128)}, f32[2,1,1,1,48,1024]{5,4,3,2,1,0:T(8,128)}, f32[1,1,1,2]{3,2,1,0:T(1,128)}, s32[1]{0:T(128)}) custom-call(f32[2,1,1,1,48,1024]{5,4,3,2,1,0:T(8,128)S(1)} %get-tuple-element.12.y, f32[2,1,1,1,48,1024]{5,4,3,2,1,0:T(8,128)S(1)} %get-tuple-element.13.c, f32[2,8,128]{2,1,0:T(8,128)S(1)} %get-tuple-element.14.residuals, ...), custom_call_target="tpu_custom_call" | custom-call | tf_op jit(solution)/shard_map/finish/pallas_call | solution.py:419

commit v3 on v2

--- a/solution.py
+++ b/solution.py
@@ -69,18 +69,15 @@
     low,
     norms,
     mine,
-    col_sums,
-    partial,
-    row_sums,
+    sums,
     sem_local,
     sem_ps,
     sem_pr,
     sem_bs,
     sem_br,
-    sem_cs,
-    sem_cr,
-    sem_rs,
-    sem_rr,
+    sem_ns,
+    sem_nr,
+    ready,
 ):
     p = lax.axis_index("prow")
     q = lax.axis_index("pcol")
@@ -115,6 +112,10 @@
     for a in range(row_tiles):
         needed = needed | (lax.rem(a * rows + p, cols) == q)
     pl.semaphore_wait(barrier, cols + rows - 2)
+    for step in range(1, rows):
+        pl.semaphore_signal(
+            ready, device_id=(lax.rem(p + step, rows), q), device_id_type=MESH
+        )
 
     def point_copy(source, target):
         return pltpu.make_async_remote_copy(
@@ -213,23 +214,16 @@
     for slot in range(1, len(slots)):
         generate(slot)
 
-    def row_copy(source, target):
+    devices = rows * cols
+    me = p * cols + q
+
+    def norm_copy(source, target):
         return pltpu.make_async_remote_copy(
             src_ref=mine,
-            dst_ref=row_sums.at[source],
-            send_sem=sem_rs.at[target],
-            recv_sem=sem_rr.at[source],
-            device_id=(target, q),
-            device_id_type=MESH,
-        )
-
-    def col_copy(source, target):
-        return pltpu.make_async_remote_copy(
-            src_ref=partial,
-            dst_ref=col_sums.at[source],
-            send_sem=sem_cs.at[target],
-            recv_sem=sem_cr.at[source],
-            device_id=(p, target),
+            dst_ref=sums.at[source],
+            send_sem=sem_ns.at[target],
+            recv_sem=sem_nr.at[source],
+            device_id=(target // cols, lax.rem(target, cols)),
             device_id_type=MESH,
         )
 
@@ -240,22 +234,23 @@
         weight = jnp.where(j < i, 2.0, 1.0).astype(F32)
         norm_sum = norm_sum + weight * all_sum(norms[slot])
         rank_sum = rank_sum + jnp.where(j < i, ranks[0, b, 0, a], 0).astype(F32)
-    first = lax.broadcasted_iota(jnp.int32, (8, 128), 0) == 0
-    mine[...] = jnp.where(first, jnp.broadcast_to(norm_sum, (8, 128)), rank_sum)
+    first = lax.broadcasted_iota(jnp.int32, (1, 128), 1) == 0
+    mine[...] = jnp.where(first, jnp.broadcast_to(norm_sum, (1, 128)), rank_sum)
 
     local[-1].wait()
     bank_copy(sibling, q, 0).wait_recv()
     for step in range(2, cols, 2):
         bank_copy(lax.rem(sibling + step, cols), q, 0).wait_recv()
 
+    pl.semaphore_wait(ready, rows - 1)
+    for step in range(1, devices):
+        norm_copy(me, lax.rem(me + step, devices)).start()
+
     def keep_of(a, b):
         return lax.broadcasted_iota(jnp.int32, (sketch_rows, 1), 0) < ranks[0, b, 0, a]
 
     for slot, (a, b) in enumerate(slots):
         i, j = place(slot)
-        if slot == 0:
-            for step in range(1, rows):
-                row_copy(p, lax.rem(p + step, rows)).start()
 
         @pl.when(j < i)
         def _():
@@ -283,13 +278,6 @@
         grams.append(gram + jnp.where(eye, diagonal, 0.0))
     inverses = invert(grams)
 
-    summed = mine[...]
-    for step in range(1, rows):
-        source = lax.rem(p + step, rows)
-        row_copy(source, p).wait_recv()
-        summed = summed + row_sums[source]
-    partial[...] = summed
-
     for slot, (a, b) in enumerate(slots):
         i, j = place(slot)
 
@@ -297,9 +285,6 @@
         def _():
             product = dot(y_out[a, 0, b, 0].astype(BF16), low[slot], 1, 0)
             c_out[a, 0, b, 0] = dot(inverses[slot], product, 1, 0, HIGH)
-
-    for step in range(1, cols):
-        col_copy(q, lax.rem(q + step, cols)).start()
 
     for slot, (a, b) in enumerate(slots):
         i, j = place(slot)
@@ -321,15 +306,15 @@
                     )
             residuals[slot] = total
 
-    whole = partial[...]
-    for step in range(1, cols):
-        source = lax.rem(q + step, cols)
-        col_copy(source, q).wait_recv()
-        whole = whole + col_sums[source]
+    whole = mine[...]
+    for step in range(1, devices):
+        source = lax.rem(me + step, devices)
+        norm_copy(source, me).wait_recv()
+        whole = whole + sums[source]
     whole_out[...] = whole
 
-    for step in range(1, cols):
-        col_copy(q, lax.rem(q + step, cols)).wait_send()
+    for step in range(1, devices):
+        norm_copy(me, lax.rem(me + step, devices)).wait_send()
 
     @pl.when(needed)
     def _():
@@ -340,8 +325,6 @@
         bank_copy(q, lax.rem(q + step, cols), step).wait_send()
         bank_copy(lax.rem(q + step, cols), sibling, cols + step).wait_send()
     bank_copy(q, sibling, 1).wait_send()
-    for step in range(1, rows):
-        row_copy(p, lax.rem(p + step, rows)).wait_send()
 
 
 def finish(rows, cols, row_tiles, col_tiles, y, c, residuals, whole, y_out, c_out, err_out, rank_out, sems):
@@ -353,7 +336,7 @@
     ]
     for copy in copies:
         copy.start()
-    norm = lax.rsqrt(whole[0:1, :]) * float(cols * col_tiles)
+    norm = lax.rsqrt(whole[0:1, 0:1]) * float(cols * col_tiles)
     lane = lax.broadcasted_iota(jnp.int32, (1, 128), 1)
     for b in range(col_tiles):
         line = jnp.zeros((1, 128), F32)
@@ -362,7 +345,7 @@
             shown = (lane == a) & (b * cols + q <= a * rows + p)
             line = jnp.where(shown, error, line)
         err_out[0, b, 0:1, :] = line[:, :row_tiles]
-    rank_out[0] = whole[1:2, 0:1].astype(jnp.int32)[0, 0]
+    rank_out[0] = whole[0:1, 1:2].astype(jnp.int32)[0, 0]
     for copy in copies:
         copy.wait()
 
@@ -385,7 +368,7 @@
             factors,
             factors,
             jax.ShapeDtypeStruct((slots, 8, 128), F32),
-            jax.ShapeDtypeStruct((8, 128), F32),
+            jax.ShapeDtypeStruct((1, 128), F32),
         ),
         in_specs=[smem, smem, hbm, hbm, hbm, hbm],
         out_specs=(vmem,) * 4,
@@ -397,19 +380,16 @@
             pltpu.VMEM((cols * per_bank, sketch_rows, size), BF16),
             pltpu.VMEM((slots, size, size), BF16),
             pltpu.VMEM((slots, 8, 128), F32),
-            pltpu.VMEM((8, 128), F32),
-            pltpu.VMEM((cols, 8, 128), F32),
-            pltpu.VMEM((8, 128), F32),
-            pltpu.VMEM((rows, 8, 128), F32),
+            pltpu.VMEM((1, 128), F32),
+            pltpu.VMEM((rows * cols, 1, 128), F32),
             dma((5,)),
             dma((cols,)),
             dma((cols,)),
             dma((2 * cols,)),
             dma((cols,)),
-            dma((cols,)),
-            dma((cols,)),
-            dma((rows,)),
-            dma((rows,)),
+            dma((rows * cols,)),
+            dma((rows * cols,)),
+            pltpu.SemaphoreType.REGULAR,
         ],
         compiler_params=pltpu.CompilerParams(
             collective_id=0, has_side_effects=True, vmem_limit_bytes=40 * 1024 * 1024

time: 28.4 us -> 26.8 us (0.944)
  Pallas kernels: 26.3 us -> 24.7 us
    pallas_call x1, Pallas kernels: 24.9 us -> 23.2 us  [per_device(): pl.pallas_call(functools.partial(kernel, rows, cols, row_tiles, col_tiles...]
where the time goes in v3:
time: 26.8 us; the launch traced here: 26.6 us
  Pallas kernels  24.7 us (92%)
  between operations  1.93 us (7%)
    pallas_call x1, Pallas kernels, per_device(): pl.pallas_call(functools.partial(kernel, rows, cols, row_tiles, col_tiles...  23.2 us
    pallas_call x1, Pallas kernels, per_device(): pl.pallas_call(functools.partial(finish, rows, cols, row_tiles, col_tiles...  1.44 us

profile of v3, /device:TPU:0, one launch (start us, length us, event | category | flops | bytes accessed | tf_op | source)
XLA Modules:
  0.0 26.6 jit_solution(17953768112852884669)
XLA Ops:
  1.9 23.2 %tiles.1 = (f32[2,1,1,1,48,1024]{5,4,3,2,1,0:T(8,128)S(1)}, f32[2,1,1,1,48,1024]{5,4,3,2,1,0:T(8,128)S(1)}, f32[2,8,128]{2,1,0:T(8,128)S(1)}, f32[1,128]{1,0:T(1,128)S(1)}) custom-call(f32[1]{0:T(128)S(6)} %copy.10.range_length, s32[1]{0:T(128)S(6)} %copy.11.smoothness, f32[1,1,2,1024]{3,2,1,0:T(2,128)} %points_hbm.1, bf16[1,48,1024]{2,1,0:T(8,128)(2,1)} %bank_hbm.1, ...), custom_call_target="tpu_custom_call" | custom-call | tf_op jit(solution)/shard_map/tiles/pallas_call | solution.py:365
  25.2 1.4 %finish.1 = (f32[2,1,1,1,48,1024]{5,4,3,2,1,0:T(8,128)}, f32[2,1,1,1,48,1024]{5,4,3,2,1,0:T(8,128)}, f32[1,1,1,2]{3,2,1,0:T(1,128)}, s32[1]{0:T(128)}) custom-call(f32[2,1,1,1,48,1024]{5,4,3,2,1,0:T(8,128)S(1)} %get-tuple-element.12.y, f32[2,1,1,1,48,1024]{5,4,3,2,1,0:T(8,128)S(1)} %get-tuple-element.13.c, f32[2,8,128]{2,1,0:T(8,128)S(1)} %get-tuple-element.14.residuals, ...), custom_call_target="tpu_custom_call" | custom-call | tf_op jit(solution)/shard_map/finish/pallas_call | solution.py:399

commit v4 on v3

--- a/solution.py
+++ b/solution.py
@@ -30,20 +30,37 @@
     return jnp.sum(jnp.sum(x, axis=1, keepdims=True), axis=0, keepdims=True)
 
 
-def invert(mats):
+def invert(mats, group=8):
     size = mats[0].shape[0]
-    row_at = lax.broadcasted_iota(jnp.int32, (size, size), 0)
-    col_at = lax.broadcasted_iota(jnp.int32, (size, size), 1)
-    for k in range(size):
-        following = []
-        for m in mats:
-            col = jnp.broadcast_to(m[:, k : k + 1], (size, size))
-            inverse = 1.0 / col[k : k + 1, :]
-            row = jnp.where(col_at[:1] == k, 1.0, m[k : k + 1, :]) * inverse
-            rest = jnp.where(col_at == k, 0.0, m) - col * row
-            following.append(jnp.where(row_at == k, row, rest))
-        mats = following
-    return mats
+    parts = size // 8
+    sub = lax.broadcasted_iota(jnp.int32, (8, size), 0)
+    lane = lax.broadcasted_iota(jnp.int32, (8, size), 1)
+    mats = [[m[8 * v : 8 * v + 8] for v in range(parts)] for m in mats]
+    for start in range(0, size, group):
+        spread = [
+            {
+                k: [jnp.broadcast_to(part[:, k : k + 1], (8, size)) for part in m]
+                for k in range(start, start + group)
+            }
+            for m in mats
+        ]
+        for k in range(start, start + group):
+            at, within = divmod(k, 8)
+            for index, (m, cols) in enumerate(zip(mats, spread)):
+                col = cols.pop(k)
+                pivot = jnp.broadcast_to(col[at][within : within + 1], (8, size))
+                inverse = 1.0 / pivot
+                for other, entry in cols.items():
+                    head = jnp.broadcast_to(entry[at][within : within + 1], (8, size)) * inverse
+                    entry = [e - c * head for e, c in zip(entry, col)]
+                    entry[at] = jnp.where(sub == within, head, entry[at])
+                    cols[other] = entry
+                row = jnp.broadcast_to(m[at][within : within + 1], (8, size))
+                row = jnp.where(lane == k, 1.0, row) * inverse
+                m = [jnp.where(lane == k, 0.0, part) - c * row for part, c in zip(m, col)]
+                m[at] = jnp.where(sub == within, row, m[at])
+                mats[index] = m
+    return [jnp.concatenate(m, axis=0) for m in mats]
 
 
 def kernel(
@@ -227,24 +244,23 @@
             device_id_type=MESH,
         )
 
-    norm_sum = jnp.zeros((1, 1), F32)
+    norm_sum = jnp.zeros((8, 128), F32)
     rank_sum = jnp.float32(0)
     for slot, (a, b) in enumerate(slots):
         i, j = place(slot)
-        weight = jnp.where(j < i, 2.0, 1.0).astype(F32)
-        norm_sum = norm_sum + weight * all_sum(norms[slot])
+        norm_sum = norm_sum + jnp.where(j < i, 2.0, 1.0).astype(F32) * norms[slot]
         rank_sum = rank_sum + jnp.where(j < i, ranks[0, b, 0, a], 0).astype(F32)
-    first = lax.broadcasted_iota(jnp.int32, (1, 128), 1) == 0
-    mine[...] = jnp.where(first, jnp.broadcast_to(norm_sum, (1, 128)), rank_sum)
+    mine[0:1, :] = jnp.sum(norm_sum, axis=0, keepdims=True)
+    mine[1:2, :] = jnp.full((1, 128), rank_sum)
+
+    pl.semaphore_wait(ready, rows - 1)
+    for step in range(1, devices):
+        norm_copy(me, lax.rem(me + step, devices)).start()
 
     local[-1].wait()
     bank_copy(sibling, q, 0).wait_recv()
     for step in range(2, cols, 2):
         bank_copy(lax.rem(sibling + step, cols), q, 0).wait_recv()
-
-    pl.semaphore_wait(ready, rows - 1)
-    for step in range(1, devices):
-        norm_copy(me, lax.rem(me + step, devices)).start()
 
     def keep_of(a, b):
         return lax.broadcasted_iota(jnp.int32, (sketch_rows, 1), 0) < ranks[0, b, 0, a]
@@ -336,7 +352,7 @@
     ]
     for copy in copies:
         copy.start()
-    norm = lax.rsqrt(whole[0:1, 0:1]) * float(cols * col_tiles)
+    norm = lax.rsqrt(all_sum(whole[0:1, :])) * float(cols * col_tiles)
     lane = lax.broadcasted_iota(jnp.int32, (1, 128), 1)
     for b in range(col_tiles):
         line = jnp.zeros((1, 128), F32)
@@ -345,7 +361,7 @@
             shown = (lane == a) & (b * cols + q <= a * rows + p)
             line = jnp.where(shown, error, line)
         err_out[0, b, 0:1, :] = line[:, :row_tiles]
-    rank_out[0] = whole[0:1, 1:2].astype(jnp.int32)[0, 0]
+    rank_out[0] = whole[1:2, 0:1].astype(jnp.int32)[0, 0]
     for copy in copies:
         copy.wait()
 
@@ -368,7 +384,7 @@
             factors,
             factors,
             jax.ShapeDtypeStruct((slots, 8, 128), F32),
-            jax.ShapeDtypeStruct((1, 128), F32),
+            jax.ShapeDtypeStruct((2, 128), F32),
         ),
         in_specs=[smem, smem, hbm, hbm, hbm, hbm],
         out_specs=(vmem,) * 4,
@@ -380,8 +396,8 @@
             pltpu.VMEM((cols * per_bank, sketch_rows, size), BF16),
             pltpu.VMEM((slots, size, size), BF16),
             pltpu.VMEM((slots, 8, 128), F32),
-            pltpu.VMEM((1, 128), F32),
-            pltpu.VMEM((rows * cols, 1, 128), F32),
+            pltpu.VMEM((2, 128), F32),
+            pltpu.VMEM((rows * cols, 2, 128), F32),
             dma((5,)),
             dma((cols,)),
             dma((cols,)),

time: 26.8 us -> 24.6 us (0.918)
  Pallas kernels: 24.7 us -> 22.5 us
    pallas_call x1, Pallas kernels: 23.2 us -> 21.1 us  [per_device(): pl.pallas_call(functools.partial(kernel, rows, cols, row_tiles, col_tiles...]
where the time goes in v4:
time: 24.6 us; the launch traced here: 24.4 us
  Pallas kernels  22.5 us (91%)
  between operations  1.93 us (8%)
    pallas_call x1, Pallas kernels, per_device(): pl.pallas_call(functools.partial(kernel, rows, cols, row_tiles, col_tiles...  21.1 us
    pallas_call x1, Pallas kernels, per_device(): pl.pallas_call(functools.partial(finish, rows, cols, row_tiles, col_tiles...  1.41 us

profile of v4, /device:TPU:0, one launch (start us, length us, event | category | flops | bytes accessed | tf_op | source)
XLA Modules:
  0.0 24.4 jit_solution(9693169053607008983)
XLA Ops:
  1.9 21.1 %tiles.1 = (f32[2,1,1,1,48,1024]{5,4,3,2,1,0:T(8,128)S(1)}, f32[2,1,1,1,48,1024]{5,4,3,2,1,0:T(8,128)S(1)}, f32[2,8,128]{2,1,0:T(8,128)S(1)}, f32[2,128]{1,0:T(2,128)S(1)}) custom-call(f32[1]{0:T(128)S(6)} %copy.10.range_length, s32[1]{0:T(128)S(6)} %copy.11.smoothness, f32[1,1,2,1024]{3,2,1,0:T(2,128)} %points_hbm.1, bf16[1,48,1024]{2,1,0:T(8,128)(2,1)} %bank_hbm.1, ...), custom_call_target="tpu_custom_call" | custom-call | tf_op jit(solution)/shard_map/tiles/pallas_call | solution.py:381
  23.0 1.4 %finish.1 = (f32[2,1,1,1,48,1024]{5,4,3,2,1,0:T(8,128)}, f32[2,1,1,1,48,1024]{5,4,3,2,1,0:T(8,128)}, f32[1,1,1,2]{3,2,1,0:T(1,128)}, s32[1]{0:T(128)}) custom-call(f32[2,1,1,1,48,1024]{5,4,3,2,1,0:T(8,128)S(1)} %get-tuple-element.12.y, f32[2,1,1,1,48,1024]{5,4,3,2,1,0:T(8,128)S(1)} %get-tuple-element.13.c, f32[2,8,128]{2,1,0:T(8,128)S(1)} %get-tuple-element.14.residuals, ...), custom_call_target="tpu_custom_call" | custom-call | tf_op jit(solution)/shard_map/finish/pallas_call | solution.py:415

commit v5 on v4

--- a/solution.py
+++ b/solution.py
@@ -177,7 +177,7 @@
 
     arrived = []
 
-    def generate(slot):
+    def generate(slot, begin=0, end=size // 128):
         i, j = place(slot)
         a = slots[slot][0]
         owner = lax.rem(a * rows + p, cols)
@@ -185,7 +185,7 @@
         for before in arrived:
             if before != a:
                 fresh = fresh & (owner != lax.rem(before * rows + p, cols))
-        if a not in arrived:
+        if a not in arrived and begin == 0:
             arrived.append(a)
 
             @pl.when(fresh)
@@ -221,15 +221,21 @@
                     total = total + jnp.sum((tile * tile).reshape(16, 8, 128), axis=0)
                 return total
 
-            norms[slot] = lax.fori_loop(0, size // 128, chunk, jnp.zeros((8, 128), F32))
-
-    generate(0)
-    for step in range(2, cols, 2):
-        block = lax.rem(q + step, cols)
-        bank_copy(block, q, 0).wait_recv()
-        bank_copy(block, sibling, cols + step).start()
-    for slot in range(1, len(slots)):
+            total = jnp.zeros((8, 128), F32) if begin == 0 else norms[slot]
+            norms[slot] = lax.fori_loop(begin, end, chunk, total)
+
+    def forward(steps):
+        for step in steps:
+            block = lax.rem(q + step, cols)
+            bank_copy(block, q, 0).wait_recv()
+            bank_copy(block, sibling, cols + step).start()
+
+    for slot in range(len(slots) - 1):
         generate(slot)
+    half = size // 256
+    generate(len(slots) - 1, 0, half)
+    forward(range(2, cols, 2))
+    generate(len(slots) - 1, half)
 
     devices = rows * cols
     me = p * cols + q
@@ -347,8 +353,9 @@
     p = lax.axis_index("prow")
     q = lax.axis_index("pcol")
     copies = [
-        pltpu.make_async_copy(y, y_out, sems.at[0]),
-        pltpu.make_async_copy(c, c_out, sems.at[1]),
+        pltpu.make_async_copy(source.at[a], target.at[a], sems.at[index, a])
+        for index, (source, target) in enumerate([(y, y_out), (c, c_out)])
+        for a in range(row_tiles)
     ]
     for copy in copies:
         copy.start()
@@ -422,7 +429,7 @@
         ),
         in_specs=[vmem] * 4,
         out_specs=(hbm, hbm, vmem, smem),
-        scratch_shapes=[dma((2,))],
+        scratch_shapes=[dma((2, row_tiles))],
         compiler_params=pltpu.CompilerParams(vmem_limit_bytes=16 * 1024 * 1024),
         name="finish",
     )(y, c, residuals, whole)

time: 24.6 us -> 24 us (0.976)
  the two profiles are of different devices: /device:TPU:0 before, /device:TPU:17 now
where the time goes in v5:
time: 24 us; the launch traced here: 23.9 us
  Pallas kernels  21.9 us (91%)
  between operations  1.93 us (8%)
    pallas_call x1, Pallas kernels, per_device(): pl.pallas_call(functools.partial(kernel, rows, cols, row_tiles, col_tiles...  20.5 us
    pallas_call x1, Pallas kernels, per_device(): pl.pallas_call(functools.partial(finish, rows, cols, row_tiles, col_tiles...  1.43 us

profile of v5, /device:TPU:17, one launch (start us, length us, event | category | flops | bytes accessed | tf_op | source)
XLA Modules:
  0.0 23.9 jit_solution(14409768328711052289)
XLA Ops:
  1.9 20.5 %tiles.1 = (f32[2,1,1,1,48,1024]{5,4,3,2,1,0:T(8,128)S(1)}, f32[2,1,1,1,48,1024]{5,4,3,2,1,0:T(8,128)S(1)}, f32[2,8,128]{2,1,0:T(8,128)S(1)}, f32[2,128]{1,0:T(2,128)S(1)}) custom-call(f32[1]{0:T(128)S(6)} %copy.10.range_length, s32[1]{0:T(128)S(6)} %copy.11.smoothness, f32[1,1,2,1024]{3,2,1,0:T(2,128)} %points_hbm.1, bf16[1,48,1024]{2,1,0:T(8,128)(2,1)} %bank_hbm.1, ...), custom_call_target="tpu_custom_call" | custom-call | tf_op jit(solution)/shard_map/tiles/pallas_call | solution.py:388
  22.4 1.4 %finish.1 = (f32[2,1,1,1,48,1024]{5,4,3,2,1,0:T(8,128)}, f32[2,1,1,1,48,1024]{5,4,3,2,1,0:T(8,128)}, f32[1,1,1,2]{3,2,1,0:T(1,128)}, s32[1]{0:T(128)}) custom-call(f32[2,1,1,1,48,1024]{5,4,3,2,1,0:T(8,128)S(1)} %get-tuple-element.12.y, f32[2,1,1,1,48,1024]{5,4,3,2,1,0:T(8,128)S(1)} %get-tuple-element.13.c, f32[2,8,128]{2,1,0:T(8,128)S(1)} %get-tuple-element.14.residuals, ...), custom_call_target="tpu_custom_call" | custom-call | tf_op jit(solution)/shard_map/finish/pallas_call | solution.py:422
